TPU v7x, 512 devices: a whole 4x4x16 slice. The times are simulated.
512 devices in a mesh: rows: 128 (over x, z_lo, y), cols: 4 (over z_hi, core).
Axes of the slice: x: 4, y: 4, z: 16 (z_hi: 2, z_lo: 8; z = z_hi * 8 + z_lo), core: 2. Of those that a mesh axis runs over, the one named last changes fastest.
Arguments:
- coords: int32 [8, 262144], P(None, ('rows', 'cols')), may hold values from 0 to 4095
- probes: float32 [64, 262144], P(None, ('rows', 'cols')), may hold values from -6 to 6
- lengthscales: float32 [8], replicated, may hold values from 0.15 to 0.25
- amplitude: float32 [1], replicated, may hold values from 0.1 to 0.3
- landmarks: float32 [254, 8, 128], replicated, may hold values from 0 to 1
- coupling: float32 [128, 128], replicated, may hold values from -0.5 to 0.5
Outputs:
- products: float32 [2, 64, 262144], P(None, None, ('rows', 'cols'))
All inputs are finite; a program needn't handle non-finite values.
Results may differ from a plain program's by a relative error of at most 0.0025.
Values may be sent and summed in bfloat16 or wider, within the bound.
No kernel may reach another device: no remote copies, remote signals or barrier semaphores. Data moves between devices by JAX's collectives and lax.ppermute only.
A program may use at most 64 MiB of HBM per device.

v0:
```python
import jax
import jax.numpy as jnp
from jax import lax
from jax.sharding import PartitionSpec as P


def over_pieces(array, axis):
    return lax.all_gather(array, axis).sum(0)


def swapped(array, axis, apart):
    return lax.ppermute(array, axis, [(i, i ^ 1 << apart) for i in range(lax.axis_size(axis))])


def pair_squares(left_points, right_points):
    squared = jnp.zeros((left_points.shape[1], right_points.shape[1]), jnp.float32)
    for component in range(left_points.shape[0]):
        offset = left_points[component][:, None] - right_points[component][None, :]
        squared = squared + offset * offset
    return squared


def on_device(coords, probes, lengthscales, amplitude, landmarks, coupling):
    highest = lax.Precision.HIGHEST
    inverse_scale = 1.0 / lengthscales
    scaled = coords.astype(jnp.float32) * (1.0 / 4096.0) * inverse_scale[:, None]
    strength = amplitude[0]
    signs_half = probes.astype(jnp.bfloat16)
    width = coords.shape[1]
    groups = lax.axis_size("cols")
    rows_index = lax.axis_index("rows")
    levels = lax.axis_size("rows").bit_length() - 1
    leaf_points = lax.all_gather(scaled, "cols", axis=1, tiled=True)
    leaf_signs = lax.all_gather(signs_half, "cols", axis=1, tiled=True)
    accumulated = jnp.zeros((2, probes.shape[0], width), jnp.float32)
    for row_block in range(groups):
        block_points = leaf_points[:, row_block * width : (row_block + 1) * width]
        block_signs = leaf_signs[:, row_block * width : (row_block + 1) * width]
        squared = pair_squares(block_points, scaled)
        kernel = strength * jnp.exp(-0.5 * squared)
        kernel_half = kernel.astype(jnp.bfloat16)
        slope_half = (kernel * squared).astype(jnp.bfloat16)
        accumulated = accumulated + jnp.stack(
            [
                jnp.dot(block_signs, kernel_half, preferred_element_type=jnp.float32),
                jnp.dot(block_signs, slope_half, preferred_element_type=jnp.float32),
            ]
        )
    result = accumulated
    factor_list = []
    dfactor_list = []
    for level in range(levels):
        depth = levels - level
        node = jnp.right_shift(rows_index, level)
        chosen = lax.dynamic_index_in_dim(landmarks, 2**depth - 2 + node, 0, keepdims=False)
        squared = pair_squares(scaled, chosen * inverse_scale[:, None])
        factor = strength * jnp.exp(-0.5 * squared)
        factor_list.append(factor)
        dfactor_list.append(factor * squared)
    factor_stack = jnp.stack(factor_list)
    dfactor_stack = jnp.stack(dfactor_list)
    own_project = jnp.einsum("pn,lnr->lpr", probes, factor_stack, precision=highest)
    own_dproject = jnp.einsum("pn,lnr->lpr", probes, dfactor_stack, precision=highest)
    projections = over_pieces(jnp.stack([own_project, own_dproject], axis=1), "cols")
    siblings = []
    pending = projections
    for level in range(levels):
        partner = swapped(pending[level:], "rows", level)
        siblings.append(partner[0])
        pending = pending.at[level + 1 :].add(partner[1:])
    for level in range(levels):
        sibling_sums = siblings[level]
        is_left = jnp.right_shift(rows_index, level) & 1 == 0
        core = jnp.where(is_left, coupling.T, coupling)
        first = jnp.dot(sibling_sums[0], core, precision=highest)
        second = jnp.dot(sibling_sums[1], core, precision=highest)
        value = jnp.dot(first, factor_stack[level].T, precision=highest)
        slope = jnp.dot(first, dfactor_stack[level].T, precision=highest) + jnp.dot(
            second, factor_stack[level].T, precision=highest
        )
        result = result + jnp.stack([value, slope])
    return result


def solution(mesh):
    in_specs = (P(None, ("rows", "cols")), P(None, ("rows", "cols")), P(), P(), P(), P())
    out_specs = P(None, None, ("rows", "cols"))
    return jax.shard_map(
        on_device, mesh=mesh, in_specs=in_specs, out_specs=out_specs, check_vma=False
    )
```

profile of v0, /device:TPU:8, one launch (start us, length us, event | category | flops | bytes accessed | tf_op | source)
XLA Modules:
  0.0 196.0 jit_solution(11825295575556073980)
XLA Ops:
  14.0 1.2 convolution_bitcast_fusion
  15.2 1.2 convolution_bitcast_fusion.1
  17.2 17.0 %all_gather.12 = f32[8,2048]{1,0:T(8,128)S(1)} all-gather(f32[8,512]{1,0:T(8,128)S(1)} %convert_multiply_fusion), channel_id=1, replica_groups=mesh['rows'=128,'cols'=4] {'cols'}, dimensions={1}, use_global_device_ids=true | all-gather | bytes 81920 | tf_op jit(solution)/shard_map/all_gather | solution.py:33
  34.3 18.0 %all_gather.13 = bf16[64,2048]{1,0:T(8,128)(2,1)S(1)} all-gather(bf16[64,512]{1,0:T(8,128)(2,1)S(1)} %convert_element_type.32), channel_id=1, replica_groups=mesh['rows'=128,'cols'=4] {'cols'}, dimensions={1}, use_global_device_ids=true | all-gather | bytes 327680 | tf_op jit(solution)/shard_map/all_gather | solution.py:34
  52.3 1.1 convolution_bitcast_fusion.3
  53.4 1.2 convolution_bitcast_fusion.2
  54.7 1.1 convolution_bitcast_fusion.5
  55.8 1.2 convolution_bitcast_fusion.4
  57.0 1.1 convolution_bitcast_fusion.7
  58.2 1.2 convolution_bitcast_fusion.6
  59.4 11.6 %all-gather.3.cloned.1.call-done = f32[28,2,64,128]{3,2,0,1:T(8,128)} async-done(((f32[7,2,64,128]{3,2,0,1:T(8,128)}), f32[28,2,64,128]{3,2,0,1:T(8,128)}) %all-gather.3.cloned.1.call-update) | async-done | bytes 1835024 | tf_op jit(solution)/shard_map/all_gather | solution.py:8
  71.1 1.7 reduce_sum.9
  72.7 3.6 %collective-permute-start = (f32[7,2,64,128]{3,2,0,1:T(8,128)S(1)}, f32[7,2,64,128]{3,2,0,1:T(8,128)S(1)}, u32[]{:S(2)}, u32[]{:S(2)}) collective-permute-start(f32[7,2,64,128]{3,2,0,1:T(8,128)S(1)} %reduce_sum.9), channel_id=1, source_target_pairs={{0,4},{4,0},{8,12},{12,8},{16,20},{20,16},{24,28},{28,24},{32,36},... | collective-permute-start | bytes 1376264 | tf_op jit(solution)/shard_map/ppermute | solution.py:12
  76.3 1.1 convolution_bitcast_fusion.9
  77.6 1.2 convolution_bitcast_fusion.8
  78.9 8.4 %collective-permute-done = f32[7,2,64,128]{3,2,0,1:T(8,128)S(1)} collective-permute-done((f32[7,2,64,128]{3,2,0,1:T(8,128)S(1)}, f32[7,2,64,128]{3,2,0,1:T(8,128)S(1)}, u32[]{:S(2)}, u32[]{:S(2)}) %collective-permute-start) | collective-permute-done | bytes 458784 | tf_op jit(solution)/shard_map/ppermute | solution.py:12
  87.3 4.4 %collective-permute-start.1 = (f32[6,2,64,128]{3,2,0,1:T(8,128)S(1)}, f32[6,2,64,128]{3,2,0,1:T(8,128)S(1)}, u32[]{:S(2)}, u32[]{:S(2)}) collective-permute-start(f32[6,2,64,128]{3,2,0,1:T(8,128)S(1)} %slice_add_fusion), channel_id=1, source_target_pairs={{0,8},{4,12},{8,0},{12,4},{16,24},{20,28},{24,16},{28,20},{32,40},... | collective-permute-start | bytes 1179656 | tf_op jit(solution)/shard_map/ppermute | solution.py:12
  94.1 1.0 fusion.6
  95.1 6.0 %collective-permute-done.1 = f32[6,2,64,128]{3,2,0,1:T(8,128)S(1)} collective-permute-done((f32[6,2,64,128]{3,2,0,1:T(8,128)S(1)}, f32[6,2,64,128]{3,2,0,1:T(8,128)S(1)}, u32[]{:S(2)}, u32[]{:S(2)}) %collective-permute-start.1) | collective-permute-done | bytes 393248 | tf_op jit(solution)/shard_map/ppermute | solution.py:12
  101.2 7.4 %collective-permute-start.2 = (f32[5,2,64,128]{3,2,0,1:T(8,128)S(1)}, f32[5,2,64,128]{3,2,0,1:T(8,128)S(1)}, u32[]{:S(2)}, u32[]{:S(2)}) collective-permute-start(f32[5,2,64,128]{3,2,0,1:T(8,128)S(1)} %slice_add_fusion.1), channel_id=1, source_target_pairs={{0,16},{4,20},{8,24},{12,28},{16,0},{20,4},{24,8},{28,12},{32,48},... | collective-permute-start | bytes 983048 | tf_op jit(solution)/shard_map/ppermute | solution.py:12
  109.0 1.0 fusion.50
  111.0 1.0 fusion.5
  112.0 3.0 %collective-permute-done.2 = f32[5,2,64,128]{3,2,0,1:T(8,128)S(1)} collective-permute-done((f32[5,2,64,128]{3,2,0,1:T(8,128)S(1)}, f32[5,2,64,128]{3,2,0,1:T(8,128)S(1)}, u32[]{:S(2)}, u32[]{:S(2)}) %collective-permute-start.2) | collective-permute-done | bytes 327712 | tf_op jit(solution)/shard_map/ppermute | solution.py:12
  115.0 7.8 %collective-permute-start.3 = (f32[4,2,64,128]{3,2,0,1:T(8,128)S(1)}, f32[4,2,64,128]{3,2,0,1:T(8,128)S(1)}, u32[]{:S(2)}, u32[]{:S(2)}) collective-permute-start(f32[4,2,64,128]{3,2,0,1:T(8,128)S(1)} %slice_add_fusion.2), channel_id=1, source_target_pairs={{0,32},{4,36},{8,40},{12,44},{16,48},{20,52},{24,56},{28,60},{32,0... | collective-permute-start | bytes 786440 | tf_op jit(solution)/shard_map/ppermute | solution.py:12
  126.2 6.7 %collective-permute-done.3 = f32[4,2,64,128]{3,2,0,1:T(8,128)S(1)} collective-permute-done((f32[4,2,64,128]{3,2,0,1:T(8,128)S(1)}, f32[4,2,64,128]{3,2,0,1:T(8,128)S(1)}, u32[]{:S(2)}, u32[]{:S(2)}) %collective-permute-start.3) | collective-permute-done | bytes 262176 | tf_op jit(solution)/shard_map/ppermute | solution.py:12
  132.8 21.1 %collective-permute-start.4 = (f32[3,2,64,128]{3,2,0,1:T(8,128)S(1)}, f32[3,2,64,128]{3,2,0,1:T(8,128)S(1)}, u32[]{:S(2)}, u32[]{:S(2)}) collective-permute-start(f32[3,2,64,128]{3,2,0,1:T(8,128)S(1)} %slice_add_fusion.3), channel_id=1, source_target_pairs={{0,64},{4,68},{8,72},{12,76},{16,80},{20,84},{24,88},{28,92},{32,9... | collective-permute-start | bytes 589832 | tf_op jit(solution)/shard_map/ppermute | solution.py:12
  154.2 1.0 fusion.46
  157.3 11.9 %collective-permute-done.4 = f32[3,2,64,128]{3,2,0,1:T(8,128)S(1)} collective-permute-done((f32[3,2,64,128]{3,2,0,1:T(8,128)S(1)}, f32[3,2,64,128]{3,2,0,1:T(8,128)S(1)}, u32[]{:S(2)}, u32[]{:S(2)}) %collective-permute-start.4) | collective-permute-done | bytes 196640 | tf_op jit(solution)/shard_map/ppermute | solution.py:12
  169.2 3.6 %collective-permute-start.5 = (f32[2,2,64,128]{3,2,0,1:T(8,128)S(1)}, f32[2,2,64,128]{3,2,0,1:T(8,128)S(1)}, u32[]{:S(2)}, u32[]{:S(2)}) collective-permute-start(f32[2,2,64,128]{3,2,0,1:T(8,128)S(1)} %slice_add_fusion.4), channel_id=1, source_target_pairs={{0,128},{4,132},{8,136},{12,140},{16,144},{20,148},{24,152},{28,15... | collective-permute-start | bytes 393224 | tf_op jit(solution)/shard_map/ppermute | solution.py:12
  176.6 4.9 %collective-permute-start.6 = (f32[1,2,64,128]{3,2,0,1:T(8,128)S(1)}, f32[1,2,64,128]{3,2,0,1:T(8,128)S(1)}, u32[]{:S(2)}, u32[]{:S(2)}) collective-permute-start(f32[1,2,64,128]{3,2,0,1:T(8,128)S(1)} %slice_add_fusion.5), channel_id=1, source_target_pairs={{0,256},{4,260},{8,264},{12,268},{16,272},{20,276},{24,280},{28,28... | collective-permute-start | bytes 196616 | tf_op jit(solution)/shard_map/ppermute | solution.py:12
  181.7 1.0 fusion.42
  188.2 1.0 fusion.39
  (64 shorter events, 26.6 us)
Async XLA Ops:
  6.5 64.5 %all-gather.3.cloned.1.call-start = ((), (), s32[]{:S(2)}) async-start(), calls=%async_computation | async-start | bytes 2293760 | tf_op jit(solution)/shard_map/all_gather | solution.py:8
  10.2 3.8 %copy-start.1 = (f32[64,512]{1,0:T(8,128)S(1)}, f32[64,512]{1,0:T(8,128)}, u32[]{:S(2)}) copy-start(f32[64,512]{1,0:T(8,128)} %param.19) | copy-start | bytes 393220
  72.7 14.5 %collective-permute-start = (f32[7,2,64,128]{3,2,0,1:T(8,128)S(1)}, f32[7,2,64,128]{3,2,0,1:T(8,128)S(1)}, u32[]{:S(2)}, u32[]{:S(2)}) collective-permute-start(f32[7,2,64,128]{3,2,0,1:T(8,128)S(1)} %reduce_sum.9), channel_id=1, source_target_pairs={{0,4},{4,0},{8,12},{12,8},{16,20},{20,16},{24,28},{28,24},{32,36},... | collective-permute-start | bytes 1376264 | tf_op jit(solution)/shard_map/ppermute | solution.py:12
  76.3 1.2 copy-start
  87.3 13.8 %collective-permute-start.1 = (f32[6,2,64,128]{3,2,0,1:T(8,128)S(1)}, f32[6,2,64,128]{3,2,0,1:T(8,128)S(1)}, u32[]{:S(2)}, u32[]{:S(2)}) collective-permute-start(f32[6,2,64,128]{3,2,0,1:T(8,128)S(1)} %slice_add_fusion), channel_id=1, source_target_pairs={{0,8},{4,12},{8,0},{12,4},{16,24},{20,28},{24,16},{28,20},{32,40},... | collective-permute-start | bytes 1179656 | tf_op jit(solution)/shard_map/ppermute | solution.py:12
  101.2 13.8 %collective-permute-start.2 = (f32[5,2,64,128]{3,2,0,1:T(8,128)S(1)}, f32[5,2,64,128]{3,2,0,1:T(8,128)S(1)}, u32[]{:S(2)}, u32[]{:S(2)}) collective-permute-start(f32[5,2,64,128]{3,2,0,1:T(8,128)S(1)} %slice_add_fusion.1), channel_id=1, source_target_pairs={{0,16},{4,20},{8,24},{12,28},{16,0},{20,4},{24,8},{28,12},{32,48},... | collective-permute-start | bytes 983048 | tf_op jit(solution)/shard_map/ppermute | solution.py:12
  115.0 17.8 %collective-permute-start.3 = (f32[4,2,64,128]{3,2,0,1:T(8,128)S(1)}, f32[4,2,64,128]{3,2,0,1:T(8,128)S(1)}, u32[]{:S(2)}, u32[]{:S(2)}) collective-permute-start(f32[4,2,64,128]{3,2,0,1:T(8,128)S(1)} %slice_add_fusion.2), channel_id=1, source_target_pairs={{0,32},{4,36},{8,40},{12,44},{16,48},{20,52},{24,56},{28,60},{32,0... | collective-permute-start | bytes 786440 | tf_op jit(solution)/shard_map/ppermute | solution.py:12
  132.8 36.4 %collective-permute-start.4 = (f32[3,2,64,128]{3,2,0,1:T(8,128)S(1)}, f32[3,2,64,128]{3,2,0,1:T(8,128)S(1)}, u32[]{:S(2)}, u32[]{:S(2)}) collective-permute-start(f32[3,2,64,128]{3,2,0,1:T(8,128)S(1)} %slice_add_fusion.3), channel_id=1, source_target_pairs={{0,64},{4,68},{8,72},{12,76},{16,80},{20,84},{24,88},{28,92},{32,9... | collective-permute-start | bytes 589832 | tf_op jit(solution)/shard_map/ppermute | solution.py:12
  169.2 7.3 %collective-permute-start.5 = (f32[2,2,64,128]{3,2,0,1:T(8,128)S(1)}, f32[2,2,64,128]{3,2,0,1:T(8,128)S(1)}, u32[]{:S(2)}, u32[]{:S(2)}) collective-permute-start(f32[2,2,64,128]{3,2,0,1:T(8,128)S(1)} %slice_add_fusion.4), channel_id=1, source_target_pairs={{0,128},{4,132},{8,136},{12,140},{16,144},{20,148},{24,152},{28,15... | collective-permute-start | bytes 393224 | tf_op jit(solution)/shard_map/ppermute | solution.py:12
  176.6 8.2 %collective-permute-start.6 = (f32[1,2,64,128]{3,2,0,1:T(8,128)S(1)}, f32[1,2,64,128]{3,2,0,1:T(8,128)S(1)}, u32[]{:S(2)}, u32[]{:S(2)}) collective-permute-start(f32[1,2,64,128]{3,2,0,1:T(8,128)S(1)} %slice_add_fusion.5), channel_id=1, source_target_pairs={{0,256},{4,260},{8,264},{12,268},{16,272},{20,276},{24,280},{28,28... | collective-permute-start | bytes 196616 | tf_op jit(solution)/shard_map/ppermute | solution.py:12
Sparse Core Ops, SparseCore 0:
  17.3 53.6 all-gather.2
where the time goes:
time: 197 us; the launch traced here: 196 us
  starting transfers between devices  52.9 us (27%)
  waiting for transfers between devices  48 us (24%)
  matrix products  35.1 us (18%)
  blocking collectives  35 us (18%)
  between operations  14.5 us (7%)
  other arithmetic  10.3 us (5%)
    ppermute x7, starting transfers between devices, swapped(): lax.ppermute(array, axis, [(i, i ^ 1 << apart) for i in range(lax.axis_si...  52.9 us
    ppermute x7, waiting for transfers between devices, swapped(): lax.ppermute(array, axis, [(i, i ^ 1 << apart) for i in range(lax.axis_si...  36.3 us
    all_gather x1, blocking collectives, on_device(): leaf_signs = lax.all_gather(signs_half, 'cols', axis=1, tiled=True)  18 us
    all_gather x1, blocking collectives, on_device(): leaf_points = lax.all_gather(scaled, 'cols', axis=1, tiled=True)  17 us
    all_gather x1, waiting for transfers between devices, over_pieces(): return lax.all_gather(array, axis).sum(0)  11.6 us
    dot_general x7, matrix products, on_device(): jnp.dot(first, dfactor_stack[level].T, precision=highest)  6.9 us
    dot_general x7, matrix products, on_device(): jnp.dot(second, factor_stack[level].T, precision=highest)  6.89 us
    dot_general x7, matrix products, on_device(): value = jnp.dot(first, factor_stack[level].T, precision=highest)  6.88 us
  transfers between devices with their start and end apart: 8, of which 7 were waited for; matrix products, arithmetic and copies ran while one was open for 15% of the time, Pallas kernels for 0%

commit v1 on v0

--- a/solution.py
+++ b/solution.py
@@ -31,7 +31,10 @@
     rows_index = lax.axis_index("rows")
     levels = lax.axis_size("rows").bit_length() - 1
     leaf_points = lax.all_gather(scaled, "cols", axis=1, tiled=True)
-    leaf_signs = lax.all_gather(signs_half, "cols", axis=1, tiled=True)
+    n_dev = lax.axis_size("cols")
+    shards = jnp.stack([signs_half for _ in range(n_dev)])
+    shards = lax.all_to_all(shards, "cols", split_axis=0, concat_axis=0)
+    leaf_signs = jnp.concatenate(shards, axis=1)
     accumulated = jnp.zeros((2, probes.shape[0], width), jnp.float32)
     for row_block in range(groups):
         block_points = leaf_points[:, row_block * width : (row_block + 1) * width]

time: 197 us -> 203 us (1.030)
  the two profiles are of different devices: /device:TPU:8 before, /device:TPU:1 now
where the time goes in v1:
time: 203 us
  waiting for transfers between devices  79.1 us (39%)
  starting transfers between devices  44.4 us (22%)
  matrix products  35.1 us (17%)
  blocking collectives  18.5 us (9%)
  between operations  14.5 us (7%)
  other arithmetic  10.4 us (5%)
    ppermute x7, waiting for transfers between devices, swapped(): lax.ppermute(array, axis, [(i, i ^ 1 << apart) for i in range(lax.axis_si...  43.6 us
    all_gather x1, waiting for transfers between devices, over_pieces(): return lax.all_gather(array, axis).sum(0)  35.5 us
    ppermute x7, starting transfers between devices, swapped(): lax.ppermute(array, axis, [(i, i ^ 1 << apart) for i in range(lax.axis_si...  27.8 us
    all_gather x1, blocking collectives, on_device(): leaf_points = lax.all_gather(scaled, 'cols', axis=1, tiled=True)  18.5 us
    all_to_all x1, starting transfers between devices, on_device(): shards = lax.all_to_all(shards, 'cols', split_axis=0, concat_axis=0)  16.6 us
    dot_general x7, matrix products, on_device(): jnp.dot(first, dfactor_stack[level].T, precision=highest)  6.9 us
    dot_general x7, matrix products, on_device(): jnp.dot(second, factor_stack[level].T, precision=highest)  6.89 us
    dot_general x7, matrix products, on_device(): value = jnp.dot(first, factor_stack[level].T, precision=highest)  6.88 us
  transfers between devices with their start and end apart: 9, of which 6 were waited for; matrix products, arithmetic and copies ran while one was open for 15% of the time, Pallas kernels for 0%

profile of v1, /device:TPU:1, one launch (start us, length us, event | category | flops | bytes accessed | tf_op | source)
XLA Modules:
  0.0 202.9 jit_solution(12443829410471080058)
XLA Ops:
  14.0 1.2 convolution_bitcast_fusion
  15.2 1.2 convolution_bitcast_fusion.1
  18.0 16.6 %all-to-all-start = ((bf16[4,64,512]{2,1,0:T(8,128)(2,1)}), bf16[4,64,512]{2,1,0:T(8,128)(2,1)S(1)}, u32[]{:S(2)}, u32[]{:S(2)}) async-start(bf16[4,64,512]{2,1,0:T(8,128)(2,1)} %stack.135), calls=%async_computation | async-start | bytes 524288 | tf_op jit(solution)/shard_map/all_to_all | solution.py:36
  34.7 18.5 %all_gather.9 = f32[8,2048]{1,0:T(8,128)S(1)} all-gather(f32[8,512]{1,0:T(8,128)S(1)} %convert_multiply_fusion), channel_id=1, replica_groups=mesh['rows'=128,'cols'=4] {'cols'}, dimensions={1}, use_global_device_ids=true | all-gather | bytes 81920 | tf_op jit(solution)/shard_map/all_gather | solution.py:33
  53.3 1.1 convolution_bitcast_fusion.3
  54.5 1.2 convolution_bitcast_fusion.2
  55.7 1.1 convolution_bitcast_fusion.5
  56.8 1.2 convolution_bitcast_fusion.4
  58.1 1.1 convolution_bitcast_fusion.7
  59.2 1.2 convolution_bitcast_fusion.6
  60.4 35.5 %all-gather.3.cloned.1.call-done = f32[28,2,64,128]{3,2,0,1:T(8,128)} async-done(((f32[7,2,64,128]{3,2,0,1:T(8,128)}), f32[28,2,64,128]{3,2,0,1:T(8,128)}) %all-gather.3.cloned.1.call-update) | async-done | bytes 1835024 | tf_op jit(solution)/shard_map/all_gather | solution.py:8
  95.9 1.7 reduce_sum.9
  97.6 1.9 collective-permute-start
  99.5 1.1 convolution_bitcast_fusion.9
  100.7 1.2 convolution_bitcast_fusion.8
  101.9 9.4 %collective-permute-done = f32[7,2,64,128]{3,2,0,1:T(8,128)S(1)} collective-permute-done((f32[7,2,64,128]{3,2,0,1:T(8,128)S(1)}, f32[7,2,64,128]{3,2,0,1:T(8,128)S(1)}, u32[]{:S(2)}, u32[]{:S(2)}) %collective-permute-start) | collective-permute-done | bytes 458784 | tf_op jit(solution)/shard_map/ppermute | solution.py:12
  111.3 5.0 %collective-permute-start.1 = (f32[6,2,64,128]{3,2,0,1:T(8,128)S(1)}, f32[6,2,64,128]{3,2,0,1:T(8,128)S(1)}, u32[]{:S(2)}, u32[]{:S(2)}) collective-permute-start(f32[6,2,64,128]{3,2,0,1:T(8,128)S(1)} %slice_add_fusion), channel_id=1, source_target_pairs={{0,8},{4,12},{8,0},{12,4},{16,24},{20,28},{24,16},{28,20},{32,40},... | collective-permute-start | bytes 1179656 | tf_op jit(solution)/shard_map/ppermute | solution.py:12
  118.7 1.0 fusion.6
  119.7 4.5 %collective-permute-done.1 = f32[6,2,64,128]{3,2,0,1:T(8,128)S(1)} collective-permute-done((f32[6,2,64,128]{3,2,0,1:T(8,128)S(1)}, f32[6,2,64,128]{3,2,0,1:T(8,128)S(1)}, u32[]{:S(2)}, u32[]{:S(2)}) %collective-permute-start.1) | collective-permute-done | bytes 393248 | tf_op jit(solution)/shard_map/ppermute | solution.py:12
  124.3 6.3 %collective-permute-start.2 = (f32[5,2,64,128]{3,2,0,1:T(8,128)S(1)}, f32[5,2,64,128]{3,2,0,1:T(8,128)S(1)}, u32[]{:S(2)}, u32[]{:S(2)}) collective-permute-start(f32[5,2,64,128]{3,2,0,1:T(8,128)S(1)} %slice_add_fusion.1), channel_id=1, source_target_pairs={{0,16},{4,20},{8,24},{12,28},{16,0},{20,4},{24,8},{28,12},{32,48},... | collective-permute-start | bytes 983048 | tf_op jit(solution)/shard_map/ppermute | solution.py:12
  133.0 1.0 fusion.5
  134.0 3.0 %collective-permute-done.2 = f32[5,2,64,128]{3,2,0,1:T(8,128)S(1)} collective-permute-done((f32[5,2,64,128]{3,2,0,1:T(8,128)S(1)}, f32[5,2,64,128]{3,2,0,1:T(8,128)S(1)}, u32[]{:S(2)}, u32[]{:S(2)}) %collective-permute-start.2) | collective-permute-done | bytes 327712 | tf_op jit(solution)/shard_map/ppermute | solution.py:12
  137.0 2.7 %collective-permute-start.3 = (f32[4,2,64,128]{3,2,0,1:T(8,128)S(1)}, f32[4,2,64,128]{3,2,0,1:T(8,128)S(1)}, u32[]{:S(2)}, u32[]{:S(2)}) collective-permute-start(f32[4,2,64,128]{3,2,0,1:T(8,128)S(1)} %slice_add_fusion.2), channel_id=1, source_target_pairs={{0,32},{4,36},{8,40},{12,44},{16,48},{20,52},{24,56},{28,60},{32,0... | collective-permute-start | bytes 786440 | tf_op jit(solution)/shard_map/ppermute | solution.py:12
  142.0 1.0 fusion.4
  143.0 9.7 %collective-permute-done.3 = f32[4,2,64,128]{3,2,0,1:T(8,128)S(1)} collective-permute-done((f32[4,2,64,128]{3,2,0,1:T(8,128)S(1)}, f32[4,2,64,128]{3,2,0,1:T(8,128)S(1)}, u32[]{:S(2)}, u32[]{:S(2)}) %collective-permute-start.3) | collective-permute-done | bytes 262176 | tf_op jit(solution)/shard_map/ppermute | solution.py:12
  152.8 4.0 %collective-permute-start.4 = (f32[3,2,64,128]{3,2,0,1:T(8,128)S(1)}, f32[3,2,64,128]{3,2,0,1:T(8,128)S(1)}, u32[]{:S(2)}, u32[]{:S(2)}) collective-permute-start(f32[3,2,64,128]{3,2,0,1:T(8,128)S(1)} %slice_add_fusion.3), channel_id=1, source_target_pairs={{0,64},{4,68},{8,72},{12,76},{16,80},{20,84},{24,88},{28,92},{32,9... | collective-permute-start | bytes 589832 | tf_op jit(solution)/shard_map/ppermute | solution.py:12
  156.9 1.0 fusion.46
  160.1 16.9 %collective-permute-done.4 = f32[3,2,64,128]{3,2,0,1:T(8,128)S(1)} collective-permute-done((f32[3,2,64,128]{3,2,0,1:T(8,128)S(1)}, f32[3,2,64,128]{3,2,0,1:T(8,128)S(1)}, u32[]{:S(2)}, u32[]{:S(2)}) %collective-permute-start.4) | collective-permute-done | bytes 196640 | tf_op jit(solution)/shard_map/ppermute | solution.py:12
  177.0 3.5 %collective-permute-start.5 = (f32[2,2,64,128]{3,2,0,1:T(8,128)S(1)}, f32[2,2,64,128]{3,2,0,1:T(8,128)S(1)}, u32[]{:S(2)}, u32[]{:S(2)}) collective-permute-start(f32[2,2,64,128]{3,2,0,1:T(8,128)S(1)} %slice_add_fusion.4), channel_id=1, source_target_pairs={{0,128},{4,132},{8,136},{12,140},{16,144},{20,148},{24,152},{28,15... | collective-permute-start | bytes 393224 | tf_op jit(solution)/shard_map/ppermute | solution.py:12
  180.7 1.0 fusion.44
  183.9 4.4 %collective-permute-start.6 = (f32[1,2,64,128]{3,2,0,1:T(8,128)S(1)}, f32[1,2,64,128]{3,2,0,1:T(8,128)S(1)}, u32[]{:S(2)}, u32[]{:S(2)}) collective-permute-start(f32[1,2,64,128]{3,2,0,1:T(8,128)S(1)} %slice_add_fusion.5), channel_id=1, source_target_pairs={{0,256},{4,260},{8,264},{12,268},{16,272},{20,276},{24,280},{28,28... | collective-permute-start | bytes 196616 | tf_op jit(solution)/shard_map/ppermute | solution.py:12
  195.0 1.0 fusion.39
  (67 shorter events, 27.0 us)
Async XLA Ops:
  6.5 89.4 %all-gather.3.cloned.1.call-start = ((), (), s32[]{:S(2)}) async-start(), calls=%async_computation.1 | async-start | bytes 2293760 | tf_op jit(solution)/shard_map/all_gather | solution.py:8
  10.2 3.8 %copy-start.1 = (f32[64,512]{1,0:T(8,128)S(1)}, f32[64,512]{1,0:T(8,128)}, u32[]{:S(2)}) copy-start(f32[64,512]{1,0:T(8,128)} %param.19) | copy-start | bytes 393220
  15.2 19.3 %copy-start = (f32[128,128]{1,0:T(8,128)S(1)}, f32[128,128]{1,0:T(8,128)}, u32[]{:S(2)}) copy-start(f32[128,128]{1,0:T(8,128)} %param.23) | copy-start | bytes 196612
  18.0 35.3 %all-to-all-start = ((bf16[4,64,512]{2,1,0:T(8,128)(2,1)}), bf16[4,64,512]{2,1,0:T(8,128)(2,1)S(1)}, u32[]{:S(2)}, u32[]{:S(2)}) async-start(bf16[4,64,512]{2,1,0:T(8,128)(2,1)} %stack.135), calls=%async_computation | async-start | bytes 524288 | tf_op jit(solution)/shard_map/all_to_all | solution.py:36
  97.6 13.7 %collective-permute-start = (f32[7,2,64,128]{3,2,0,1:T(8,128)S(1)}, f32[7,2,64,128]{3,2,0,1:T(8,128)S(1)}, u32[]{:S(2)}, u32[]{:S(2)}) collective-permute-start(f32[7,2,64,128]{3,2,0,1:T(8,128)S(1)} %reduce_sum.9), channel_id=1, source_target_pairs={{0,4},{4,0},{8,12},{12,8},{16,20},{20,16},{24,28},{28,24},{32,36},... | collective-permute-start | bytes 1376264 | tf_op jit(solution)/shard_map/ppermute | solution.py:12
  111.3 12.9 %collective-permute-start.1 = (f32[6,2,64,128]{3,2,0,1:T(8,128)S(1)}, f32[6,2,64,128]{3,2,0,1:T(8,128)S(1)}, u32[]{:S(2)}, u32[]{:S(2)}) collective-permute-start(f32[6,2,64,128]{3,2,0,1:T(8,128)S(1)} %slice_add_fusion), channel_id=1, source_target_pairs={{0,8},{4,12},{8,0},{12,4},{16,24},{20,28},{24,16},{28,20},{32,40},... | collective-permute-start | bytes 1179656 | tf_op jit(solution)/shard_map/ppermute | solution.py:12
  124.3 12.7 %collective-permute-start.2 = (f32[5,2,64,128]{3,2,0,1:T(8,128)S(1)}, f32[5,2,64,128]{3,2,0,1:T(8,128)S(1)}, u32[]{:S(2)}, u32[]{:S(2)}) collective-permute-start(f32[5,2,64,128]{3,2,0,1:T(8,128)S(1)} %slice_add_fusion.1), channel_id=1, source_target_pairs={{0,16},{4,20},{8,24},{12,28},{16,0},{20,4},{24,8},{28,12},{32,48},... | collective-permute-start | bytes 983048 | tf_op jit(solution)/shard_map/ppermute | solution.py:12
  137.0 15.7 %collective-permute-start.3 = (f32[4,2,64,128]{3,2,0,1:T(8,128)S(1)}, f32[4,2,64,128]{3,2,0,1:T(8,128)S(1)}, u32[]{:S(2)}, u32[]{:S(2)}) collective-permute-start(f32[4,2,64,128]{3,2,0,1:T(8,128)S(1)} %slice_add_fusion.2), channel_id=1, source_target_pairs={{0,32},{4,36},{8,40},{12,44},{16,48},{20,52},{24,56},{28,60},{32,0... | collective-permute-start | bytes 786440 | tf_op jit(solution)/shard_map/ppermute | solution.py:12
  152.8 24.2 %collective-permute-start.4 = (f32[3,2,64,128]{3,2,0,1:T(8,128)S(1)}, f32[3,2,64,128]{3,2,0,1:T(8,128)S(1)}, u32[]{:S(2)}, u32[]{:S(2)}) collective-permute-start(f32[3,2,64,128]{3,2,0,1:T(8,128)S(1)} %slice_add_fusion.3), channel_id=1, source_target_pairs={{0,64},{4,68},{8,72},{12,76},{16,80},{20,84},{24,88},{28,92},{32,9... | collective-permute-start | bytes 589832 | tf_op jit(solution)/shard_map/ppermute | solution.py:12
  177.0 6.8 %collective-permute-start.5 = (f32[2,2,64,128]{3,2,0,1:T(8,128)S(1)}, f32[2,2,64,128]{3,2,0,1:T(8,128)S(1)}, u32[]{:S(2)}, u32[]{:S(2)}) collective-permute-start(f32[2,2,64,128]{3,2,0,1:T(8,128)S(1)} %slice_add_fusion.4), channel_id=1, source_target_pairs={{0,128},{4,132},{8,136},{12,140},{16,144},{20,148},{24,152},{28,15... | collective-permute-start | bytes 393224 | tf_op jit(solution)/shard_map/ppermute | solution.py:12
  183.9 7.8 %collective-permute-start.6 = (f32[1,2,64,128]{3,2,0,1:T(8,128)S(1)}, f32[1,2,64,128]{3,2,0,1:T(8,128)S(1)}, u32[]{:S(2)}, u32[]{:S(2)}) collective-permute-start(f32[1,2,64,128]{3,2,0,1:T(8,128)S(1)} %slice_add_fusion.5), channel_id=1, source_target_pairs={{0,256},{4,260},{8,264},{12,268},{16,272},{20,276},{24,280},{28,28... | collective-permute-start | bytes 196616 | tf_op jit(solution)/shard_map/ppermute | solution.py:12
Sparse Core Ops, SparseCore 0:
  17.3 78.5 all-gather.2
